TPU v7x, 256 devices: a whole 4x4x8 slice. The times are simulated.
256 devices in a mesh: aa: 8 (over y, core), ba: 4 (over x), col: 8 (over z).
Axes of the slice: x: 4, y: 4, z: 8, core: 2. Of those that a mesh axis runs over, the one named last changes fastest.
Arguments:
- hidden: bfloat16 [8, 4, 32, 8192], P('aa', 'ba', None, 'col'), may hold values from -36 to 60, as said below
- unembed: bfloat16 [8192, 152064], P(None, ('aa', 'ba', 'col')), may hold values from -1 to 5, as said below
- targets: int32 [8, 4, 32], replicated, may hold values from 0 to 152063
- lengths: int32 [8, 4], replicated, may hold values from 1 to 32
Outputs:
- scores: float32 [8, 4], P('aa', 'ba')
Inputs may be any that keep to these rules, and one draw needn't show every extreme that they name: real-valued hidden states. `unembed`: real-valued unembedding entries.
All inputs are finite; a program needn't handle non-finite values.
Results may differ from a plain program's by a relative error of at most 0.0003.
Values may be sent and summed in bfloat16 or wider, within the bound.
A program may use at most 128 MiB of HBM per device.

v0:
```python
import jax
import jax.numpy as jnp
from jax import lax
from jax.sharding import Mesh
from jax.sharding import PartitionSpec as P

AA = ("aa_0", "aa_1")
AA_BA_COL = ("aa_0", "aa_1", "ba", "col")
AA_BA = ("aa_0", "aa_1", "ba")


def in_order(parts, dim):
    parts = jnp.moveaxis(parts, 0, dim)
    dims = parts.shape
    return parts.reshape(*dims[:dim], dims[dim] * dims[dim + 1], *dims[dim + 2 :])


def copy_for_each(x, axis):
    copies = jnp.broadcast_to(x, (lax.axis_size(axis), *x.shape))
    return lax.all_to_all(copies, axis, split_axis=0, concat_axis=0, tiled=True)


def gather_directly(x, axis, dim):
    return in_order(copy_for_each(x, axis), dim)


def gathered_once(x, axis):
    leaves = jax.tree.leaves(x)
    turns = sorted(range(len(leaves)), key=lambda k: -leaves[k].size)
    width = (1, *leaves[turns[0]].shape)[-1]
    lines = [
        jnp.pad(leaves[k].reshape(-1), (0, -leaves[k].size % width)).reshape(-1, width)
        for k in turns
    ]
    both, at, found = (lax.all_gather(jnp.concatenate(lines), axis), 0, {})
    for k, line in zip(turns, lines):
        slab = both[:, at : at + len(line)].reshape(len(both), -1)
        found[k] = slab[:, : leaves[k].size].reshape(-1, *leaves[k].shape)
        at += len(line)
    numbers = iter(range(len(leaves)))
    return jax.tree.map(lambda _: found[next(numbers)], x)


def merged_by_axis(x, axes, combine):
    for axis in axes:
        pieces = gathered_once(x, axis)
        x = jax.tree.map(lambda part: part[0], pieces)
        for k in range(1, lax.axis_size(axis)):
            x = combine(x, jax.tree.map(lambda part: part[k], pieces))
    return x


def combine_stats(earlier, later):
    top_one, total_one, picked_one = earlier
    top_two, total_two, picked_two = later
    joined = jnp.maximum(top_one, top_two)
    total = total_one * jnp.exp(top_one - joined) + total_two * jnp.exp(top_two - joined)
    return (joined, total, picked_one + picked_two)


def body(hidden, unembed, targets, lengths):
    groups = lax.axis_size(AA)
    members = lax.axis_size("ba")
    per_group, choices_dev, seq_len, width_part = hidden.shape
    block_rows = per_group * choices_dev * seq_len
    own_rows = hidden.reshape(block_rows, width_part)
    vocab_part = unembed.shape[1]
    device_index = lax.axis_index(AA_BA_COL)
    offset = device_index * vocab_part
    full_rows = gather_directly(own_rows, "col", 1)
    logits = jnp.dot(
        lax.all_gather(full_rows, AA_BA, axis=0, tiled=True),
        unembed,
        preferred_element_type=jnp.float32,
    )
    ordered = targets.reshape(groups, per_group, members, seq_len).transpose(0, 2, 1, 3).reshape(-1)
    local_ids = ordered - offset
    columns = jnp.arange(vocab_part, dtype=jnp.int32)
    picked_part = jnp.sum(jnp.where(local_ids[:, None] == columns[None, :], logits, 0.0), axis=1)
    group_index = lax.axis_index(AA)
    member_index = lax.axis_index("ba")
    own_len = lax.dynamic_slice(lengths, (group_index * per_group, member_index), (per_group, 1))
    positions = jnp.arange(seq_len, dtype=jnp.int32)
    local_top = jnp.max(logits, axis=1)
    relative = jnp.sum(jnp.exp(logits - local_top[:, None]), axis=1)
    top, total, picked = merged_by_axis(
        (local_top, relative, picked_part), AA_BA_COL, combine_stats
    )
    first = (group_index * members + member_index) * block_rows
    mine = lax.dynamic_slice_in_dim(picked - top - jnp.log(total), first, block_rows).reshape(
        per_group, seq_len
    )
    valid = positions[None, :] < own_len
    summed = jnp.sum(jnp.where(valid, mine, 0.0), axis=1)
    return (summed / own_len[:, 0].astype(jnp.float32))[:, None]


def solution(mesh):
    split = Mesh(
        mesh.devices.reshape(4, 2, mesh.shape["ba"], mesh.shape["col"]),
        ("aa_0", "aa_1", "ba", "col"),
    )
    in_specs = (P(AA, "ba", None, "col"), P(None, AA_BA_COL), P(), P())
    out_specs = P(AA, "ba")
    return jax.shard_map(body, mesh=split, in_specs=in_specs, out_specs=out_specs, check_vma=False)
```

profile of v0, /device:TPU:2, one launch (start us, length us, event | category | flops | bytes accessed | tf_op | source)
XLA Modules:
  0.0 185.8 jit_solution(12175652836842939492)
XLA Ops:
  6.5 0.0 copy-start
  6.5 0.0 all-gather.10.cloned.1.call-start
  6.5 0.9 broadcast_in_dim.18
  7.4 25.8 %all_to_all.5 = bf16[8,32,1024]{2,1,0:T(8,128)(2,1)S(1)} all-to-all(bf16[8,32,1024]{2,1,0:T(8,128)(2,1)S(1)} %broadcast_in_dim.18), channel_id=1, replica_groups=mesh['aa_0'=4,'aa_1'=2,'ba'=4,'col'=8] {'col'}, dimensions={0} | all-to-all | bytes 1048576 | tf_op jit(solution)/shard_map/all_to_all | solution.py:20
  33.2 0.8 copy.6
  34.0 0.0 all-gather.10.cloned.1.call-update
  34.1 0.0 copy-done
  34.1 0.1 sub.213
  34.2 1.3 dynamic_slice.6
  36.1 72.0 %all-gather.10.cloned.1.call-done = bf16[1024,8192]{1,0:T(8,128)(2,1)} async-done(((bf16[32,8192]{1,0:T(8,128)(2,1)}), bf16[1024,8192]{1,0:T(8,128)(2,1)}) %all-gather.10.cloned.1.call-update) | async-done | bytes 16777232 | tf_op jit(solution)/shard_map/all_gather | solution.py:72
  108.1 15.5 %fusion.49 = (f32[1024]{0:T(1024)S(1)}, f32[1024,594]{0,1:T(8,128)S(1)}) fusion(bf16[1024,8192]{1,0:T(8,128)(2,1)} %all-gather.10.cloned.1.call-done, bf16[8192,594]{0,1:T(8,128)(2,1)} %param.5), kind=kOutput, calls=%fused_computation.97 | convolution fusion | flops 9966273536 | bytes 28946432 | tf_op jit(solution)/shard_map/dot_general | solution.py:71
  123.6 0.7 exponential_reduce_fusion
  124.3 11.9 %all-gather.4 = f32[4,3,1024]{2,1,0:T(4,128)S(1)} all-gather(f32[1,3,1024]{2,1,0:T(4,128)S(1)} %maximum_bitcast_fusion), channel_id=2, replica_groups=mesh['aa_0'=4,'aa_1'=2,'ba'=4,'col'=8] {'aa_0'}, dimensions={0}, use_global_device_ids=true | all-gather | bytes 61440 | tf_op jit(solution)/shard_map/all_gather | solution.py:35
  136.2 0.1 fusion.16
  136.3 1.8 all-gather.5
  138.2 11.8 %all-gather.6 = f32[4,3,1024]{2,1,0:T(4,128)S(1)} all-gather(f32[1,3,1024]{2,1,0:T(4,128)S(1)} %maximum_bitcast_fusion.2), channel_id=4, replica_groups=mesh['aa_0'=4,'aa_1'=2,'ba'=4,'col'=8] {'ba'}, dimensions={0}, use_global_device_ids=true | all-gather | bytes 61440 | tf_op jit(solution)/shard_map/all_gather | solution.py:35
  150.1 0.1 fusion.2
  150.2 26.1 %all-gather.7 = f32[8,3,1024]{2,1,0:T(4,128)S(1)} all-gather(f32[1,3,1024]{2,1,0:T(4,128)S(1)} %maximum_bitcast_fusion.3), channel_id=5, replica_groups=mesh['aa_0'=4,'aa_1'=2,'ba'=4,'col'=8] {'col'}, dimensions={0}, use_global_device_ids=true | all-gather | bytes 110592 | tf_op jit(solution)/shard_map/all_gather | solution.py:35
  176.2 0.1 fusion.47
  176.3 1.4 fusion.43
  (11 shorter events, 0.2 us)
Async XLA Ops:
  6.5 27.5 %copy-start = (s32[8,4,32]{2,1,0:T(4,128)S(1)}, s32[8,4,32]{2,1,0:T(4,128)}, u32[]{:S(2)}) copy-start(s32[8,4,32]{2,1,0:T(4,128)} %param.6) | copy-start | bytes 12292
  6.5 101.5 %all-gather.10.cloned.1.call-start = ((), (), s32[]{:S(2)}) async-start(), calls=%async_computation.1 | async-start | bytes 17301504 | tf_op jit(solution)/shard_map/all_gather | solution.py:72
Sparse Core Ops, SparseCore 0:
  34.2 73.8 all-gather.9
where the time goes:
time: 186 us
  blocking collectives  77.4 us (42%)
  waiting for transfers between devices  72 us (39%)
  matrix products  15.5 us (8%)
  between operations  15.4 us (8%)
  local copies, waits for them, and re-layouts  3.1 us (2%)
  other arithmetic  2.39 us (1%)
    all_gather x1, waiting for transfers between devices, body(): lax.all_gather(full_rows, AA_BA, axis=0, tiled=True)  72 us
    all_gather x4, blocking collectives, gathered_once(): both, at, found = (lax.all_gather(jnp.concatenate(lines), axis), 0, {})  51.6 us
    all_to_all x1, blocking collectives, copy_for_each(): return lax.all_to_all(copies, axis, split_axis=0, concat_axis=0, tiled=True)  25.8 us
    dot_general x1, matrix products, body(): jnp.dot(lax.all_gather(full_rows, AA_BA, axis=0, tiled=True), unembed, pr...  15.5 us
  transfers between devices with their start and end apart: 1, of which 1 were waited for; matrix products, arithmetic and copies ran while one was open for 1% of the time, Pallas kernels for 0%

commit v1 on v0

--- a/solution.py
+++ b/solution.py
@@ -7,6 +7,13 @@
 AA = ("aa_0", "aa_1")
 AA_BA_COL = ("aa_0", "aa_1", "ba", "col")
 AA_BA = ("aa_0", "aa_1", "ba")
+
+
+def all_by_exchange(x, mesh_axis, d):
+    size = lax.axis_size(mesh_axis)
+    blocks = jnp.stack([x for _ in range(size)])
+    blocks = lax.all_to_all(blocks, mesh_axis, split_axis=0, concat_axis=0)
+    return jnp.concatenate(blocks, axis=d)
 
 
 def in_order(parts, dim):
@@ -69,9 +76,7 @@
     offset = device_index * vocab_part
     full_rows = gather_directly(own_rows, "col", 1)
     logits = jnp.dot(
-        lax.all_gather(full_rows, AA_BA, axis=0, tiled=True),
-        unembed,
-        preferred_element_type=jnp.float32,
+        all_by_exchange(full_rows, AA_BA, 0), unembed, preferred_element_type=jnp.float32
     )
     ordered = targets.reshape(groups, per_group, members, seq_len).transpose(0, 2, 1, 3).reshape(-1)
     local_ids = ordered - offset

time: 186 us -> 329 us (1.77)
  waiting for transfers between devices: 72 us -> 216 us
  between operations: 15.4 us -> 1.99 us
  starting transfers between devices: 0.01 us -> 7.8 us
  local copies, waits for them, and re-layouts: 3.1 us -> 8.27 us
    all_to_all x0 -> x1, waiting for transfers between devices: none -> 216 us  [all_by_exchange(): blocks = lax.all_to_all(blocks, mesh_axis, split_axis=0, concat_axis=0)]
    all_gather x1 -> x0, waiting for transfers between devices: 72 us -> none  [body(): lax.all_gather(full_rows, AA_BA, axis=0, tiled=True)]
    all_to_all x0 -> x1, starting transfers between devices: none -> 7.8 us  [all_by_exchange(): blocks = lax.all_to_all(blocks, mesh_axis, split_axis=0, concat_axis=0)]
    another operation x0 -> x2, local copies, waits for them, and re-layouts: none -> 6.01 us  [all_by_exchange(): blocks = jnp.stack([x for _ in range(size)])]
  transfers between devices with their start and end apart: 1 -> 1, of which waited for: 1 -> 1; matrix products, arithmetic and copies ran while one was open for 1% -> 0% of each run, Pallas kernels for 0% -> 0%
where the time goes in v1:
time: 329 us; the launch traced here: 327 us
  waiting for transfers between devices  216 us (66%)
  blocking collectives  75.1 us (23%)
  matrix products  15.5 us (5%)
  local copies, waits for them, and re-layouts  8.27 us (3%)
  starting transfers between devices  7.8 us (2%)
    all_to_all x1, waiting for transfers between devices, all_by_exchange(): blocks = lax.all_to_all(blocks, mesh_axis, split_axis=0, concat_axis=0)  216 us
    all_gather x4, blocking collectives, gathered_once(): both, at, found = (lax.all_gather(jnp.concatenate(lines), axis), 0, {})  49.3 us
    all_to_all x1, blocking collectives, copy_for_each(): return lax.all_to_all(copies, axis, split_axis=0, concat_axis=0, tiled=True)  25.8 us
    dot_general x1, matrix products, body(): jnp.dot(all_by_exchange(full_rows, AA_BA, 0), unembed, preferred_element_...  15.5 us
    all_to_all x1, starting transfers between devices, all_by_exchange(): blocks = lax.all_to_all(blocks, mesh_axis, split_axis=0, concat_axis=0)  7.8 us
  transfers between devices with their start and end apart: 1, of which 1 were waited for; matrix products, arithmetic and copies ran while one was open for 0% of the time, Pallas kernels for 0%

profile of v1, /device:TPU:2, one launch (start us, length us, event | category | flops | bytes accessed | tf_op | source)
XLA Modules:
  0.0 326.6 jit_solution(11175913170780034391)
XLA Ops:
  0.0 0.9 broadcast_in_dim.18
  0.9 25.8 %all_to_all.10 = bf16[8,32,1024]{2,1,0:T(8,128)(2,1)S(1)} all-to-all(bf16[8,32,1024]{2,1,0:T(8,128)(2,1)S(1)} %broadcast_in_dim.18), channel_id=1, replica_groups=mesh['aa_0'=4,'aa_1'=2,'ba'=4,'col'=8] {'col'}, dimensions={0} | all-to-all | bytes 1048576 | tf_op jit(solution)/shard_map/all_to_all | solution.py:27
  26.7 6.0 %stack.3 = bf16[32,32,8192]{2,1,0:T(8,128)(2,1)} broadcast(bf16[32,8192]{1,0:T(8,128)(2,1)S(1)} %bitcast.217), dimensions={1,2} | broadcast | bytes 17301504 | tf_op jit(solution)/shard_map/stack | solution.py:14
  32.7 0.0 copy-start
  32.7 7.8 %all-to-all-start.1 = ((bf16[32,32,8192]{2,1,0:T(8,128)(2,1)}), bf16[32,32,8192]{2,1,0:T(8,128)(2,1)}, u32[]{:S(2)}, u32[]{:S(2)}) async-start(bf16[32,32,8192]{2,1,0:T(8,128)(2,1)} %stack.3), calls=%async_computation.1 | async-start | bytes 33554432 | tf_op jit(solution)/shard_map/all_to_all | solution.py:15
  40.5 0.0 copy-done
  40.5 0.1 sub.213
  40.6 1.3 dynamic_slice.6
  42.5 215.5 %all-to-all-done.1 = bf16[32,32,8192]{2,1,0:T(8,128)(2,1)} async-done(((bf16[32,32,8192]{2,1,0:T(8,128)(2,1)}), bf16[32,32,8192]{2,1,0:T(8,128)(2,1)}, u32[]{:S(2)}, u32[]{:S(2)}) %all-to-all-start.1) | async-done | bytes 16777248 | tf_op jit(solution)/shard_map/all_to_all | solution.py:15
  258.1 15.5 %fusion.49 = (f32[1024]{0:T(1024)S(1)}, f32[1024,594]{0,1:T(8,128)S(1)}) fusion(bf16[1024,8192]{1,0:T(8,128)(2,1)} %bitcast.3, bf16[8192,594]{0,1:T(8,128)(2,1)} %param.5), kind=kOutput, calls=%fused_computation.97 | convolution fusion | flops 9966273536 | bytes 28946432 | tf_op jit(solution)/shard_map/dot_general | solution.py:78
  273.6 0.7 exponential_reduce_fusion
  274.3 12.2 %all-gather.4 = f32[4,3,1024]{2,1,0:T(4,128)S(1)} all-gather(f32[1,3,1024]{2,1,0:T(4,128)S(1)} %maximum_bitcast_fusion), channel_id=2, replica_groups=mesh['aa_0'=4,'aa_1'=2,'ba'=4,'col'=8] {'aa_0'}, dimensions={0}, use_global_device_ids=true | all-gather | bytes 61440 | tf_op jit(solution)/shard_map/all_gather | solution.py:42
  286.5 0.1 fusion.16
  286.6 1.8 all-gather.5
  288.5 10.7 %all-gather.6 = f32[4,3,1024]{2,1,0:T(4,128)S(1)} all-gather(f32[1,3,1024]{2,1,0:T(4,128)S(1)} %maximum_bitcast_fusion.2), channel_id=4, replica_groups=mesh['aa_0'=4,'aa_1'=2,'ba'=4,'col'=8] {'ba'}, dimensions={0}, use_global_device_ids=true | all-gather | bytes 61440 | tf_op jit(solution)/shard_map/all_gather | solution.py:42
  299.2 0.1 fusion.2
  299.3 24.6 %all-gather.7 = f32[8,3,1024]{2,1,0:T(4,128)S(1)} all-gather(f32[1,3,1024]{2,1,0:T(4,128)S(1)} %maximum_bitcast_fusion.3), channel_id=5, replica_groups=mesh['aa_0'=4,'aa_1'=2,'ba'=4,'col'=8] {'col'}, dimensions={0}, use_global_device_ids=true | all-gather | bytes 110592 | tf_op jit(solution)/shard_map/all_gather | solution.py:42
  323.9 0.1 fusion.47
  324.0 1.4 fusion.43
  (12 shorter events, 0.2 us)
Async XLA Ops:
  32.7 7.8 %copy-start = (s32[8,4,32]{2,1,0:T(4,128)S(1)}, s32[8,4,32]{2,1,0:T(4,128)}, u32[]{:S(2)}) copy-start(s32[8,4,32]{2,1,0:T(4,128)} %param.6) | copy-start | bytes 12292
  32.7 225.4 %all-to-all-start.1 = ((bf16[32,32,8192]{2,1,0:T(8,128)(2,1)}), bf16[32,32,8192]{2,1,0:T(8,128)(2,1)}, u32[]{:S(2)}, u32[]{:S(2)}) async-start(bf16[32,32,8192]{2,1,0:T(8,128)(2,1)} %stack.3), calls=%async_computation.1 | async-start | bytes 33554432 | tf_op jit(solution)/shard_map/all_to_all | solution.py:15
